TPU v7x, 32 devices: a whole 2x2x4 slice. The times are simulated.
32 devices in a mesh: dp: 4 (over y, x), ctx: 4 (over z), tensor: 2 (over core).
Axes of the slice: x: 2, y: 2, z: 4, core: 2. Of those that a mesh axis runs over, the one named last changes fastest.
Arguments:
- block_input: bfloat16 [4, 2048, 1536], P('dp', 'ctx'), may hold values from -6 to 6
- segments: int32 [4, 2048], P('dp'), may hold values from 0 to 31, as said below
- positions: int32 [4, 2048], P('dp', 'ctx'), may hold values from 0 to 1023, as said below
- cotangent: bfloat16 [4, 2048, 1536], P('dp', 'ctx'), may hold values from -6 to 6
- norm1_gain: float32 [1536], replicated, may hold values from 0.1 to 1.9
- w_query: bfloat16 [1536, 1536], P(None, 'tensor'), may hold values from -0.15625 to 0.15625
- w_key: bfloat16 [1536, 768], P(None, 'tensor'), may hold values from -0.15625 to 0.15625
- w_value: bfloat16 [1536, 768], P(None, 'tensor'), may hold values from -0.15625 to 0.15625
- w_out: bfloat16 [1536, 1536], P('tensor'), may hold values from -0.625 to 0.625
- norm2_gain: float32 [1536], replicated, may hold values from 0.1 to 1.9
- w_gate: bfloat16 [1536, 4096], P(None, 'tensor'), may hold values from -0.15625 to 0.15625
- w_up: bfloat16 [1536, 4096], P(None, 'tensor'), may hold values from -0.15625 to 0.15625
- w_down: bfloat16 [4096, 1536], P('tensor'), may hold values from -0.09375 to 0.09375
Outputs:
- block_output: bfloat16 [4, 2048, 1536], P('dp', 'ctx')
- grad_input: bfloat16 [4, 2048, 1536], P('dp', 'ctx')
- grad_norm1: float32 [1536], replicated
- grad_query: float32 [1536, 1536], P(None, 'tensor')
- grad_key: float32 [1536, 768], P(None, 'tensor')
- grad_value: float32 [1536, 768], P(None, 'tensor')
- grad_out: float32 [1536, 1536], P('tensor')
- grad_norm2: float32 [1536], replicated
- grad_gate: float32 [1536, 4096], P(None, 'tensor')
- grad_up: float32 [1536, 4096], P(None, 'tensor')
- grad_down: float32 [4096, 1536], P('tensor')
Inputs may be any that keep to these rules, and one draw needn't show every extreme that they name: `segments`: along each sequence the document numbers start at 0, never fall, rise by at most one at a time and only at multiples of 64 positions; every document spans at most 1024 positions. `positions`: each token's position counted from the start of its document.
All inputs are finite; a program needn't handle non-finite values.
Results may differ from a plain program's by a relative error of at most 0.025.
Values may be sent and summed in bfloat16 or wider, within the bound.
A program may use at most 320 MiB of HBM per device.

v0:
```python
import jax
import jax.numpy as jnp
from jax import lax
from jax.sharding import PartitionSpec as P

HDIM = 96
EPSILON = 1e-05
THETA_BASE = 100000.0
MASKED_SCORE = -1e30


def rotate(tensor_in, where, sign):
    half = tensor_in.shape[-1] // 2
    freqs = THETA_BASE ** (-(jnp.arange(half, dtype=jnp.float32) * 2.0) / tensor_in.shape[-1])
    angles = where.astype(jnp.float32)[..., None] * freqs
    cosine = jnp.cos(angles)[..., None, :]
    sine = sign * jnp.sin(angles)[..., None, :]
    first = tensor_in[..., :half]
    second = tensor_in[..., half:]
    return jnp.concatenate(
        [first * cosine - second * sine, second * cosine + first * sine], axis=-1
    )


def tdot(left, right):
    return lax.dot_general(
        left, right, (((0,), (0,)), ((), ())), preferred_element_type=jnp.float32
    )


def rdot(left, right):
    return lax.dot_general(
        left, right, (((1,), (1,)), ((), ())), preferred_element_type=jnp.float32
    )


def masked_scores(query_rows, kv_rows, seg_query, seg_keys, query_index, heads_kv, scale):
    length = kv_rows.shape[0]
    kv_width = kv_rows.shape[1] // 2
    key_all = kv_rows[:, :kv_width].reshape(length, heads_kv, -1)
    value_all = kv_rows[:, kv_width:].reshape(length, heads_kv, -1)
    raw_scores = (
        jnp.einsum("qkgd,skd->kgqs", query_rows, key_all, preferred_element_type=jnp.float32)
        * scale
    )
    allowed = (seg_query[:, None] == seg_keys[None, :]) & (
        jnp.arange(length, dtype=jnp.int32)[None, :] <= query_index[:, None]
    )
    return (jnp.where(allowed, raw_scores, MASKED_SCORE), key_all, value_all)


def shards(
    block_input,
    segments,
    positions,
    cotangent,
    norm1_gain,
    w_query,
    w_key,
    w_value,
    w_out,
    norm2_gain,
    w_gate,
    w_up,
    w_down,
):
    seq_count, stretch_len, width_all = block_input.shape
    length = segments.shape[1]
    heads_q = w_query.shape[1] // HDIM
    heads_kv = w_key.shape[1] // HDIM
    group = heads_q // heads_kv
    kv_width = w_key.shape[1]
    row_count = seq_count * stretch_len
    scale = HDIM ** (-0.5)
    qblock = min(512, stretch_len)
    nblocks = stretch_len // qblock
    offset = lax.axis_index("ctx") * stretch_len
    inputs = block_input.reshape(row_count, width_all).astype(jnp.float32)
    inv_one = lax.rsqrt(jnp.mean(inputs * inputs, axis=1, keepdims=True) + EPSILON)
    normed1 = (inputs * inv_one * norm1_gain).astype(jnp.bfloat16)
    queries = rotate(
        jnp.dot(normed1, w_query, preferred_element_type=jnp.float32).reshape(
            seq_count, stretch_len, heads_q, HDIM
        ),
        positions,
        1.0,
    ).astype(jnp.bfloat16)
    keys = rotate(
        jnp.dot(normed1, w_key, preferred_element_type=jnp.float32).reshape(
            seq_count, stretch_len, heads_kv, HDIM
        ),
        positions,
        1.0,
    ).astype(jnp.bfloat16)
    values = jnp.dot(normed1, w_value, preferred_element_type=jnp.float32).astype(jnp.bfloat16)
    local_kv = jnp.concatenate(
        [
            keys.reshape(seq_count, stretch_len, kv_width),
            values.reshape(seq_count, stretch_len, kv_width),
        ],
        axis=2,
    )
    whole_kv = lax.all_gather(local_kv, "ctx", axis=1, tiled=True)

    def forward_block(item):
        seq_id = item // nblocks
        start = item % nblocks * qblock
        query_rows = lax.dynamic_index_in_dim(queries, seq_id, 0, keepdims=False).reshape(
            qblock, heads_kv, group, HDIM
        )
        seg_row = lax.dynamic_index_in_dim(segments, seq_id, 0, keepdims=False)
        seg_query = lax.dynamic_slice_in_dim(seg_row, offset + start, qblock, 0)
        query_index = offset + start + jnp.arange(qblock, dtype=jnp.int32)
        kv_rows = lax.dynamic_index_in_dim(whole_kv, seq_id, 0, keepdims=False)
        scores, key_all, value_all = masked_scores(
            query_rows, kv_rows, seg_query, seg_row, query_index, heads_kv, scale
        )
        row_max = jnp.max(scores, axis=-1)
        log_total = row_max + jnp.log(jnp.sum(jnp.exp(scores - row_max[..., None]), axis=-1))
        probs = jnp.exp(scores - log_total[..., None]).astype(jnp.bfloat16)
        block_out = jnp.einsum(
            "kgqs,skd->qkgd", probs, value_all, preferred_element_type=jnp.float32
        )
        return (block_out.reshape(qblock, heads_q * HDIM).astype(jnp.bfloat16), log_total)

    outs_blocks, log_totals = lax.map(
        forward_block, jnp.arange(seq_count * nblocks, dtype=jnp.int32)
    )
    attended = outs_blocks.reshape(row_count, heads_q * HDIM)
    log_totals = log_totals.reshape(seq_count, nblocks, heads_kv, group, qblock)
    attn_branch = lax.psum(
        jnp.dot(attended, w_out, preferred_element_type=jnp.float32).astype(jnp.bfloat16), "tensor"
    ).astype(jnp.float32)
    hidden = inputs + attn_branch
    inv_two = lax.rsqrt(jnp.mean(hidden * hidden, axis=1, keepdims=True) + EPSILON)
    normed2 = (hidden * inv_two * norm2_gain).astype(jnp.bfloat16)
    gate = jnp.dot(normed2, w_gate, preferred_element_type=jnp.float32)
    upper = jnp.dot(normed2, w_up, preferred_element_type=jnp.float32)
    sigmoid_gate = jax.nn.sigmoid(gate)
    activated = gate * sigmoid_gate
    mixed = (activated * upper).astype(jnp.bfloat16)
    ffn_branch = lax.psum(
        jnp.dot(mixed, w_down, preferred_element_type=jnp.float32).astype(jnp.bfloat16), "tensor"
    ).astype(jnp.float32)
    block_output = (
        (hidden + ffn_branch).astype(jnp.bfloat16).reshape(seq_count, stretch_len, width_all)
    )
    grad_rows_out = cotangent.reshape(row_count, width_all)
    grad_wdown = tdot(mixed, grad_rows_out)
    grad_mixed = rdot(grad_rows_out, w_down)
    grad_gate_act = (
        grad_mixed * upper * sigmoid_gate * (1.0 + gate * (1.0 - sigmoid_gate))
    ).astype(jnp.bfloat16)
    grad_upper = (grad_mixed * activated).astype(jnp.bfloat16)
    grad_wgate = tdot(normed2, grad_gate_act)
    grad_wup = tdot(normed2, grad_upper)
    grad_normed2 = lax.psum(
        (rdot(grad_gate_act, w_gate) + rdot(grad_upper, w_up)).astype(jnp.bfloat16), "tensor"
    ).astype(jnp.float32)
    scaled_two = grad_normed2 * norm2_gain
    grad_gain_two = jnp.sum(grad_normed2 * hidden * inv_two, axis=0)
    grad_hidden = (
        grad_rows_out.astype(jnp.float32)
        + inv_two * scaled_two
        - hidden
        * (inv_two * inv_two * inv_two)
        * jnp.mean(scaled_two * hidden, axis=1, keepdims=True)
    )
    grad_branch = grad_hidden.astype(jnp.bfloat16)
    grad_wout = tdot(attended, grad_branch)
    grad_attended = rdot(grad_branch, w_out).astype(jnp.bfloat16)
    attended_seq = attended.reshape(seq_count, stretch_len, heads_q * HDIM)
    grad_att_seq = grad_attended.reshape(seq_count, stretch_len, heads_q * HDIM)

    def backward_seq(seq_id):
        kv_rows = lax.dynamic_index_in_dim(whole_kv, seq_id, 0, keepdims=False)
        seg_row = lax.dynamic_index_in_dim(segments, seq_id, 0, keepdims=False)
        query_seq = lax.dynamic_index_in_dim(queries, seq_id, 0, keepdims=False)
        out_seq = lax.dynamic_index_in_dim(attended_seq, seq_id, 0, keepdims=False)
        grad_seq = lax.dynamic_index_in_dim(grad_att_seq, seq_id, 0, keepdims=False)
        log_seq = lax.dynamic_index_in_dim(log_totals, seq_id, 0, keepdims=False)

        def backward_block(carry, block_id):
            start = block_id * qblock
            query_rows = query_seq.reshape(qblock, heads_kv, group, HDIM)
            out_rows = out_seq.reshape(qblock, heads_kv, group, HDIM)
            grad_rows = grad_seq.reshape(qblock, heads_kv, group, HDIM)
            seg_query = lax.dynamic_slice_in_dim(seg_row, offset + start, qblock, 0)
            query_index = offset + start + jnp.arange(qblock, dtype=jnp.int32)
            scores, key_all, value_all = masked_scores(
                query_rows, kv_rows, seg_query, seg_row, query_index, heads_kv, scale
            )
            log_total = lax.dynamic_index_in_dim(log_seq, block_id, 0, keepdims=False)
            probs = jnp.exp(scores - log_total[..., None])
            probs_half = probs.astype(jnp.bfloat16)
            delta = jnp.sum(
                grad_rows.astype(jnp.float32) * out_rows.astype(jnp.float32), axis=3
            ).transpose(1, 2, 0)
            grad_probs = jnp.einsum(
                "qkgd,skd->kgqs", grad_rows, value_all, preferred_element_type=jnp.float32
            )
            grad_scores = (probs * (grad_probs - delta[..., None])).astype(jnp.bfloat16)
            grad_q = (
                jnp.einsum(
                    "kgqs,skd->qkgd", grad_scores, key_all, preferred_element_type=jnp.float32
                )
                * scale
            )
            grad_k = (
                jnp.einsum(
                    "kgqs,qkgd->skd", grad_scores, query_rows, preferred_element_type=jnp.float32
                )
                * scale
            )
            grad_v = jnp.einsum(
                "kgqs,qkgd->skd", probs_half, grad_rows, preferred_element_type=jnp.float32
            )
            added = jnp.concatenate(
                [grad_k.reshape(length, kv_width), grad_v.reshape(length, kv_width)], axis=1
            )
            return (carry + added, grad_q.reshape(qblock, heads_q * HDIM))

        kv_total, grad_q_blocks = lax.scan(
            backward_block,
            jnp.zeros((length, 2 * kv_width), jnp.float32),
            jnp.arange(nblocks, dtype=jnp.int32),
        )
        return (grad_q_blocks.reshape(stretch_len, heads_q * HDIM), kv_total)

    grad_q_all, grad_kv_all = lax.map(backward_seq, jnp.arange(seq_count, dtype=jnp.int32))
    grad_kv_local = lax.psum_scatter(
        grad_kv_all.astype(jnp.bfloat16), "ctx", scatter_dimension=1, tiled=True
    ).astype(jnp.float32)
    grad_keys = (
        rotate(
            grad_kv_local[:, :, :kv_width].reshape(seq_count, stretch_len, heads_kv, HDIM),
            positions,
            -1.0,
        )
        .astype(jnp.bfloat16)
        .reshape(row_count, kv_width)
    )
    grad_values = grad_kv_local[:, :, kv_width:].astype(jnp.bfloat16).reshape(row_count, kv_width)
    grad_queries = (
        rotate(grad_q_all.reshape(seq_count, stretch_len, heads_q, HDIM), positions, -1.0)
        .astype(jnp.bfloat16)
        .reshape(row_count, heads_q * HDIM)
    )
    grad_wquery = tdot(normed1, grad_queries)
    grad_wkey = tdot(normed1, grad_keys)
    grad_wvalue = tdot(normed1, grad_values)
    grad_normed1 = lax.psum(
        (rdot(grad_queries, w_query) + rdot(grad_keys, w_key) + rdot(grad_values, w_value)).astype(
            jnp.bfloat16
        ),
        "tensor",
    ).astype(jnp.float32)
    scaled_one = grad_normed1 * norm1_gain
    grad_gain_one = jnp.sum(grad_normed1 * inputs * inv_one, axis=0)
    grad_in = (
        grad_hidden
        + inv_one * scaled_one
        - inputs
        * (inv_one * inv_one * inv_one)
        * jnp.mean(scaled_one * inputs, axis=1, keepdims=True)
    ).astype(jnp.bfloat16)
    grad_in = grad_in.reshape(seq_count, stretch_len, width_all)
    (
        grad_gain_one,
        grad_wquery,
        grad_wkey,
        grad_wvalue,
        grad_wout,
        grad_gain_two,
        grad_wgate,
        grad_wup,
        grad_wdown,
    ) = (
        lax.psum(grad_gain_one.astype(jnp.bfloat16), ("dp", "ctx")).astype(jnp.float32),
        lax.psum(grad_wquery.astype(jnp.bfloat16), ("dp", "ctx")).astype(jnp.float32),
        lax.psum(grad_wkey.astype(jnp.bfloat16), ("dp", "ctx")).astype(jnp.float32),
        lax.psum(grad_wvalue.astype(jnp.bfloat16), ("dp", "ctx")).astype(jnp.float32),
        lax.psum(grad_wout.astype(jnp.bfloat16), ("dp", "ctx")).astype(jnp.float32),
        lax.psum(grad_gain_two.astype(jnp.bfloat16), ("dp", "ctx")).astype(jnp.float32),
        lax.psum(grad_wgate.astype(jnp.bfloat16), ("dp", "ctx")).astype(jnp.float32),
        lax.psum(grad_wup.astype(jnp.bfloat16), ("dp", "ctx")).astype(jnp.float32),
        lax.psum(grad_wdown.astype(jnp.bfloat16), ("dp", "ctx")).astype(jnp.float32),
    )
    return (
        block_output,
        grad_in,
        grad_gain_one,
        grad_wquery,
        grad_wkey,
        grad_wvalue,
        grad_wout,
        grad_gain_two,
        grad_wgate,
        grad_wup,
        grad_wdown,
    )


def solution(mesh):
    placed = (
        P("dp", "ctx", None),
        P("dp", None),
        P("dp", "ctx"),
        P("dp", "ctx", None),
        P(),
        P(None, "tensor"),
        P(None, "tensor"),
        P(None, "tensor"),
        P("tensor", None),
        P(),
        P(None, "tensor"),
        P(None, "tensor"),
        P("tensor", None),
    )
    return jax.shard_map(
        shards,
        mesh=mesh,
        in_specs=placed,
        out_specs=(
            P("dp", "ctx", None),
            P("dp", "ctx", None),
            P(),
            P(None, "tensor"),
            P(None, "tensor"),
            P(None, "tensor"),
            P("tensor", None),
            P(),
            P(None, "tensor"),
            P(None, "tensor"),
            P("tensor", None),
        ),
        check_vma=False,
    )
```

profile of v0, /device:TPU:0, one launch (start us, length us, event | category | flops | bytes accessed | tf_op | source)
XLA Modules:
  0.0 1100.4 jit_solution(7658305326652356975)
XLA Ops:
  18.7 4.3 copy.32
  23.0 3.6 fusion.51
  28.7 56.0 %all-gather.2.cloned.1.call-done = bf16[1,2048,768]{1,2,0:T(8,128)(2,1)} async-done(((bf16[1,512,768]{1,2,0:T(8,128)(2,1)}), bf16[1,2048,768]{1,2,0:T(8,128)(2,1)}) %all-gather.2.cloned.1.call-update) | async-done | bytes 3145744 | tf_op jit(solution)/shard_map/all_gather | solution.py:103
  87.0 13.8 %fusion.3 = (f32[4,2,512]{2,1,0:T(2,128)S(1)}, f32[4,2048,512,2]{2,1,3,0:T(8,128)}) fusion(pred[512,2048]{0,1:T(8,128)(4,1)S(1)} %fusion.5, bf16[2048,4,96,1]{0,2,3,1:T(8,128)(2,1)S(1)} %bitcast.198, bf16[512,4,2,48]{0,3,2,1:T(8,128)(2,1)S(1)} %bitcast.221, bf16[512,4,2,48]{0,3,2,1:T(8,128)(2,1)S(1)} %bitcast.219), kind=kOutput, calls=%fused_computation.7 | convolution fusion | flops 1637347328 | bytes 36978688 | tf_op jit(solution)/shard_map/while/body/eval_jaxpr/qkgd,skd->kgqs/dot_general | solution.py:43
  100.8 14.4 %exponential_reduce_fusion = f32[4,2,512]{2,1,0:T(2,128)S(1)} fusion(f32[4,2048,512,2]{2,1,3,0:T(8,128)} %get-tuple-element.140, f32[4,2,512]{2,1,0:T(2,128)S(1)} %get-tuple-element.139, pred[512,2048]{0,1:T(8,128)(4,1)S(1)} %fusion.5), kind=kLoop, calls=%fused_computation.5 | loop fusion | flops 33550336 | bytes 34635776 | tf_op jit(solution)/shard_map/while/body/eval_jaxpr/reduce_sum | solution.py:119
  115.2 15.0 %convolution_convert_fusion.10 = bf16[4,96,2,512]{3,1,2,0:T(8,128)(2,1)S(1)} fusion(bf16[2048,4,96,1]{0,2,3,1:T(8,128)(2,1)S(1)} %bitcast.215, f32[4,2048,512,2]{2,1,3,0:T(8,128)} %get-tuple-element.140, f32[4,2,512]{2,1,0:T(2,128)S(1)} %bitcast.230, pred[512,2048]{0,1:T(8,128)(4,1)S(1)} %fusion.5), kind=kOutput, calls=%fused_computation.87 | convolution fusion | flops 1644560384 | bytes 36978688 | tf_op jit(solution)/shard_map/while/body/eval_jaxpr/kgqs,skd->qkgd/dot_general | solution.py:121
  134.1 18.7 %all-reduce.8.cloned.1.call-done = bf16[512,1536]{1,0:T(8,128)(2,1)} async-done(((bf16[512,1536]{1,0:T(8,128)(2,1)}), bf16[512,1536]{1,0:T(8,128)(2,1)}) %all-reduce.8.cloned.1.call-update) | async-done | bytes 1572880 | tf_op jit(solution)/shard_map/psum | solution.py:131
  156.3 6.5 fusion.77
  162.8 4.9 fusion.76
  167.8 10.1 multiply_convert_fusion
  177.9 5.2 fusion.78
  183.1 7.6 fusion.34
  190.9 21.5 %all-reduce.10.cloned.1.call-done = bf16[512,1536]{1,0:T(8,128)(2,1)} async-done(((bf16[512,1536]{1,0:T(8,128)(2,1)}), bf16[512,1536]{1,0:T(8,128)(2,1)}) %all-reduce.10.cloned.1.call-update) | async-done | bytes 1572880 | tf_op jit(solution)/shard_map/psum | solution.py:157
  212.4 3.7 fusion.22
  225.6 15.2 %bitcast_convert_fusion = bf16[4,96,2048]{2,1,0:T(8,128)(2,1)} fusion(bf16[512,4,2,96]{0,3,2,1:T(8,128)(2,1)S(1)} %bitcast.210, f32[4,2048,512,2]{2,1,3,0:T(8,128)} %get-tuple-element.140, f32[4,2,512]{2,1,0:T(2,128)S(1)} %bitcast.231, pred[512,2048]{0,1:T(8,128)(4,1)S(1)} %fusion.5), kind=kOutput, calls=%fused_computation.55 | convolution fusion | flops 1644953600 | bytes 36978688 | tf_op jit(solution)/shard_map/while/body/eval_jaxpr/while/body/eval_jaxpr/kgqs,qkgd->skd/dot_general | solution.py:215
  240.8 20.1 %fusion.1 = bf16[4,2,512,2048]{2,3,1,0:T(8,128)(2,1)} fusion(f32[4,2048,512,2]{2,1,3,0:T(8,128)} %get-tuple-element.140, bf16[2048,4,96,1]{0,2,3,1:T(8,128)(2,1)S(1)} %bitcast.216, bf16[512,4,2,96]{0,3,2,1:T(8,128)(2,1)S(1)} %bitcast.211, f32[4,2,512]{2,1,0:T(2,128)S(1)} %bitcast.229, f32[4,2,512]{2,1,0:T(2,128)S(1)} %bitcast.232, ...), kind=kOutput, calls=%fused_computation.2 | convolution fusion | flops 1660944384 | bytes 53772288 | tf_op jit(solution)/shard_map/while/body/eval_jaxpr/while/body/eval_jaxpr/qkgd,skd->kgqs/dot_general | solution.py:199
  260.9 11.2 %fusion.32 = bf16[4,96,2048]{2,1,0:T(8,128)(2,1)S(1)} fusion(bf16[4,2,512,2048]{2,3,1,0:T(8,128)(2,1)} %fusion.1, bf16[512,4,2,48]{0,3,2,1:T(8,128)(2,1)} %bitcast.220, bf16[512,4,2,48]{0,3,2,1:T(8,128)(2,1)} %bitcast.218), kind=kOutput, calls=%fused_computation.57 | convolution fusion | flops 1613758464 | bytes 19136512 | tf_op jit(solution)/shard_map/while/body/eval_jaxpr/while/body/eval_jaxpr/kgqs,qkgd->skd/dot_general | solution.py:210
  272.1 3.5 pad_maximum_fusion
  275.9 8.1 convolution_convert_fusion.5
  284.0 8.5 convolution_multiply_fusion
  294.5 3.1 fusion.79
  297.6 39.8 %reduce-scatter.2.cloned.1.call-done = bf16[1,512,768]{1,2,0:T(8,128)(2,1)} async-done(((bf16[1,2048,768]{1,2,0:T(8,128)(2,1)}), bf16[1,512,768]{1,2,0:T(8,128)(2,1)}) %reduce-scatter.2.cloned.1.call-update) | async-done | bytes 786448 | tf_op jit(solution)/shard_map/reduce_scatter | solution.py:231
  345.4 7.1 convolution_convert_fusion.1
  352.5 5.3 convolution_convert_fusion.2
  357.9 5.4 convolution_convert_fusion
  376.2 45.2 %all-reduce = (bf16[1536]{0:T(1024)(128)(2,1)S(1)}, bf16[1536]{0:T(1024)(128)(2,1)S(1)}) all-reduce(bf16[1536]{0:T(1024)(128)(2,1)S(1)} %get-tuple-element.94, bf16[1536]{0:T(1024)(128)(2,1)S(1)} %get-tuple-element.92), channel_id=1, replica_groups=mesh['dp'=4,'ctx'=4,'tensor'=2] {'dp','ctx'}, use_global_device_ids=true, to_apply=%region_13.14 | all-reduce | flops 3072 | bytes 12288 | tf_op jit(solution)/shard_map/psum | solution.py:279
  422.6 5.6 fusion.38
  428.1 632.3 %all-reduce.12.cloned.1.call-done = (bf16[1536,768]{1,0:T(8,128)(2,1)}, bf16[1536,384]{1,0:T(8,128)(2,1)}, bf16[1536,384]{1,0:T(8,128)(2,1)}, bf16[768,1536]{1,0...) async-done(((bf16[1536,768]{1,0:T(8,128)(2,1)}, bf16[1536,384]{1,0:T(8,128)(2,1)}, bf16[1536,384]{1,0:T(8,128)(2,1)}, ...) | async-done | bytes 25952272 | tf_op jit(solution)/shard_map/psum | solution.py:280
  1060.4 4.3 convert_element_type.284
  1071.0 9.2 convert_element_type.294
  1080.2 6.3 convert_element_type.296
  1086.5 6.6 convert_element_type.298
  (165 shorter events, 63.2 us)
Async XLA Ops:
  7.2 123.9 %copy-start = (bf16[768,1536]{1,0:T(8,128)(2,1)S(1)}, bf16[768,1536]{1,0:T(8,128)(2,1)}, u32[]{:S(2)}) copy-start(bf16[768,1536]{1,0:T(8,128)(2,1)} %param.21) | copy-start | bytes 7077892
  7.2 77.5 %all-gather.2.cloned.1.call-start = ((), (), s32[]{:S(2)}) async-start(), calls=%async_computation.1 | async-start | bytes 3932160 | tf_op jit(solution)/shard_map/all_gather | solution.py:103
  10.9 12.1 %copy-start.38 = (f32[512]{0:T(512)}, f32[512]{0:T(512)S(1)}, u32[]{:S(2)}) copy-start(f32[512]{0:T(512)S(1)} %get-tuple-element.136) | copy-start | bytes 6148
  17.3 9.3 copy-start.16
  18.4 134.4 %all-reduce.8.cloned.1.call-start = ((), (), s32[]{:S(2)}) async-start(), calls=%async_computation.2 | async-start | bytes 3145728 | tf_op jit(solution)/shard_map/psum | solution.py:131
  86.9 13.8 %copy-start.10 = (bf16[2048,384]{0,1:T(8,128)(2,1)}, bf16[2048,384]{0,1:T(8,128)(2,1)S(1)}, u32[]{:S(2)}) copy-start(bf16[2048,384]{0,1:T(8,128)(2,1)S(1)} %get-tuple-element.120) | copy-start | bytes 4718596
  86.9 28.3 %copy-start.22 = (bf16[2048,384]{0,1:T(8,128)(2,1)}, bf16[2048,384]{0,1:T(8,128)(2,1)S(1)}, u32[]{:S(2)}) copy-start(bf16[2048,384]{0,1:T(8,128)(2,1)S(1)} %get-tuple-element.121) | copy-start | bytes 4718596
  133.6 21.8 %copy-start.35 = (f32[1536]{0:T(1024)S(1)}, f32[1536]{0:T(1024)}, u32[]{:S(2)}) copy-start(f32[1536]{0:T(1024)} %param.22) | copy-start | bytes 18436
  133.7 78.8 %all-reduce.10.cloned.1.call-start = ((), (), s32[]{:S(2)}) async-start(), calls=%async_computation.3 | async-start | bytes 3145728 | tf_op jit(solution)/shard_map/psum | solution.py:157
  155.7 7.1 slice-start.4
  156.2 6.5 copy-start.20
  156.3 6.5 slice-start.5
  190.7 146.7 %reduce-scatter.2.cloned.1.call-start = ((), (), s32[]{:S(2)}) async-start(), calls=%async_computation.4 | async-start | bytes 3932160 | tf_op jit(solution)/shard_map/reduce_scatter | solution.py:231
  225.6 15.3 %copy-start.23 = (bf16[2048,384]{0,1:T(8,128)(2,1)S(1)}, bf16[2048,384]{0,1:T(8,128)(2,1)}, u32[]{:S(2)}) copy-start(bf16[2048,384]{0,1:T(8,128)(2,1)} %copy-done.22) | copy-start | bytes 4718596
  275.6 98.0 %all-reduce.14.cloned.1.call-start = ((), (), s32[]{:S(2)}) async-start(), calls=%async_computation.6 | async-start | bytes 6291456 | tf_op jit(solution)/shard_map/psum | solution.py:142
  275.9 8.1 copy-start.11
  284.0 8.5 copy-start.17
  284.0 8.5 copy-start.31
  297.6 41.1 %copy-start.13 = (bf16[1536,384]{1,0:T(8,128)(2,1)S(1)}, bf16[1536,384]{1,0:T(8,128)(2,1)}, u32[]{:S(2)}) copy-start(bf16[1536,384]{1,0:T(8,128)(2,1)} %param.19) | copy-start | bytes 3538948
  344.0 716.4 %all-reduce.12.cloned.1.call-start = ((), (), s32[]{:S(2)}) async-start(), calls=%async_computation.5 | async-start | bytes 51904512 | tf_op jit(solution)/shard_map/psum | solution.py:280
  345.4 7.1 copy-start.43
  352.5 5.4 copy-start.45
  357.9 5.4 copy-start.5
  357.9 5.4 copy-start.34
  357.9 5.4 copy-start.37
  357.9 5.4 copy-start.39
  373.6 49.0 %copy-start.41 = (f32[512]{0:T(512)S(1)}, f32[512]{0:T(512)}, u32[]{:S(2)}) copy-start(f32[512]{0:T(512)} %get-tuple-element.135) | copy-start | bytes 6148
  1068.0 12.2 %slice-start.2 = ((s8[6291456]{0:T(1024)(128)(4,1)}), s8[4194304]{0:T(1024)(128)(4,1)S(1)}, s32[]{:S(2)}) async-start(s8[6291456]{0:T(1024)(128)(4,1)} %bitcast.204), calls=%async_computation.9 | async-start | bytes 8388608
  1071.0 9.3 slice-start.3
  1071.0 15.6 %slice-start = ((s8[6291456]{0:T(1024)(128)(4,1)}), s8[4194304]{0:T(1024)(128)(4,1)S(1)}, s32[]{:S(2)}) async-start(s8[6291456]{0:T(1024)(128)(4,1)} %bitcast.202), calls=%async_computation.7 | async-start | bytes 8388608
  1080.2 6.3 slice-start.1
  1086.5 6.6 copy-start.1
  (26 other events, 78.5 us)
Sparse Core Ops, SparseCore 0:
  18.5 66.1 all-gather.1
  133.8 18.9 all-reduce.7
  190.8 21.5 all-reduce.9
  275.8 61.5 reduce-scatter.1
  344.1 23.2 all-reduce.13
  374.9 685.5 all-reduce.11
where the time goes:
time: 1100 us
  waiting for transfers between devices  768 us (70%)
  matrix products  175 us (16%)
  other arithmetic  79.1 us (7%)
  blocking collectives  45.2 us (4%)
  local copies, waits for them, and re-layouts  16.3 us (1%)
  between operations  15.2 us (1%)
    psum x1, waiting for transfers between devices, shards(): lax.psum(grad_wquery.astype(jnp.bfloat16), ('dp', 'ctx'))  632 us
    all_gather x1, waiting for transfers between devices, shards(): whole_kv = lax.all_gather(local_kv, 'ctx', axis=1, tiled=True)  56 us
    psum x1, blocking collectives, shards(): lax.psum(grad_gain_one.astype(jnp.bfloat16), ('dp', 'ctx'))  45.2 us
    reduce_scatter x1, waiting for transfers between devices, shards(): lax.psum_scatter(grad_kv_all.astype(jnp.bfloat16), 'ctx', scatter_dimensi...  39.8 us
    dot_general x7, matrix products, rdot(): lax.dot_general(left, right, (((1,), (1,)), ((), ())), preferred_element_...  33.6 us
    dot_general x7, matrix products, tdot(): lax.dot_general(left, right, (((0,), (0,)), ((), ())), preferred_element_...  28 us
  transfers between devices with their start and end apart: 6, of which 5 were waited for; matrix products, arithmetic and copies ran while one was open for 6% of the time, Pallas kernels for 0%

commit v1 on v0

--- a/solution.py
+++ b/solution.py
@@ -2,6 +2,7 @@
 import jax.numpy as jnp
 from jax import lax
 from jax.sharding import PartitionSpec as P
+from jax.lax import all_gather
 
 HDIM = 96
 EPSILON = 1e-05
@@ -277,7 +278,7 @@
         grad_wdown,
     ) = (
         lax.psum(grad_gain_one.astype(jnp.bfloat16), ("dp", "ctx")).astype(jnp.float32),
-        lax.psum(grad_wquery.astype(jnp.bfloat16), ("dp", "ctx")).astype(jnp.float32),
+        all_gather(grad_wquery.astype(jnp.bfloat16), ("dp", "ctx")).sum(axis=0).astype(jnp.float32),
         lax.psum(grad_wkey.astype(jnp.bfloat16), ("dp", "ctx")).astype(jnp.float32),
         lax.psum(grad_wvalue.astype(jnp.bfloat16), ("dp", "ctx")).astype(jnp.float32),
         lax.psum(grad_wout.astype(jnp.bfloat16), ("dp", "ctx")).astype(jnp.float32),

time: 1100 us -> 1420 us (1.29)
  waiting for transfers between devices: 768 us -> 1070 us
  other arithmetic: 79.1 us -> 95.6 us
    all_gather x0 -> x1, waiting for transfers between devices: none -> 362 us  [shards(): all_gather(grad_wquery.astype(jnp.bfloat16), ('dp', 'ctx')).sum(axis=0)]
    psum x1, waiting for transfers between devices: 632 us -> 568 us  [shards(): lax.psum(grad_wkey.astype(jnp.bfloat16), ('dp', 'ctx')).astype(jnp.float32)]
    reduce_sum x0 -> x1, other arithmetic: none -> 14.8 us  [shards(): all_gather(grad_wquery.astype(jnp.bfloat16), ('dp', 'ctx')).sum(axis=0)]
  transfers between devices with their start and end apart: 6 -> 7, of which waited for: 5 -> 6; matrix products, arithmetic and copies ran while one was open for 6% -> 7% of each run, Pallas kernels for 0% -> 0%
where the time goes in v1:
time: 1420 us
  waiting for transfers between devices  1070 us (75%)
  matrix products  175 us (12%)
  other arithmetic  95.6 us (7%)
  blocking collectives  45.3 us (3%)
  local copies, waits for them, and re-layouts  17 us (1%)
  between operations  14.9 us (1%)
    psum x1, waiting for transfers between devices, shards(): lax.psum(grad_wkey.astype(jnp.bfloat16), ('dp', 'ctx')).astype(jnp.float32)  568 us
    all_gather x1, waiting for transfers between devices, shards(): all_gather(grad_wquery.astype(jnp.bfloat16), ('dp', 'ctx')).sum(axis=0)  362 us
    all_gather x1, waiting for transfers between devices, shards(): whole_kv = lax.all_gather(local_kv, 'ctx', axis=1, tiled=True)  56 us
    psum x1, blocking collectives, shards(): lax.psum(grad_gain_one.astype(jnp.bfloat16), ('dp', 'ctx'))  45.3 us
    reduce_scatter x1, waiting for transfers between devices, shards(): lax.psum_scatter(grad_kv_all.astype(jnp.bfloat16), 'ctx', scatter_dimensi...  39.8 us
    dot_general x7, matrix products, rdot(): lax.dot_general(left, right, (((1,), (1,)), ((), ())), preferred_element_...  33.6 us
  transfers between devices with their start and end apart: 7, of which 6 were waited for; matrix products, arithmetic and copies ran while one was open for 7% of the time, Pallas kernels for 0%

profile of v1, /device:TPU:0, one launch (start us, length us, event | category | flops | bytes accessed | tf_op | source)
XLA Modules:
  0.0 1415.3 jit_solution(16786642829205806621)
XLA Ops:
  18.8 4.3 copy.32
  23.1 3.6 fusion.51
  28.8 56.0 %all-gather.4.cloned.1.call-done = bf16[1,2048,768]{1,2,0:T(8,128)(2,1)} async-done(((bf16[1,512,768]{1,2,0:T(8,128)(2,1)}), bf16[1,2048,768]{1,2,0:T(8,128)(2,1)}) %all-gather.4.cloned.1.call-update) | async-done | bytes 3145744 | tf_op jit(solution)/shard_map/all_gather | solution.py:104
  87.0 13.8 fusion.3
  100.8 14.4 %exponential_reduce_fusion = f32[4,2,512]{2,1,0:T(2,128)S(1)} fusion(f32[4,2048,512,2]{2,1,3,0:T(8,128)} %get-tuple-element.139, f32[4,2,512]{2,1,0:T(2,128)S(1)} %get-tuple-element.138, pred[512,2048]{0,1:T(8,128)(4,1)S(1)} %fusion.5), kind=kLoop, calls=%fused_computation.5 | loop fusion | flops 33550336 | bytes 34635776 | tf_op jit(solution)/shard_map/while/body/eval_jaxpr/reduce_sum | solution.py:120
  115.2 15.0 %convolution_convert_fusion.10 = bf16[4,96,2,512]{3,1,2,0:T(8,128)(2,1)S(1)} fusion(bf16[2048,4,96,1]{0,2,3,1:T(8,128)(2,1)S(1)} %bitcast.217, f32[4,2048,512,2]{2,1,3,0:T(8,128)} %get-tuple-element.139, f32[4,2,512]{2,1,0:T(2,128)S(1)} %bitcast.232, pred[512,2048]{0,1:T(8,128)(4,1)S(1)} %fusion.5), kind=kOutput, calls=%fused_computation.87 | convolution fusion | flops 1644560384 | bytes 36978688 | tf_op jit(solution)/shard_map/while/body/eval_jaxpr/kgqs,skd->qkgd/dot_general | solution.py:122
  134.3 18.6 %all-reduce.8.cloned.1.call-done = bf16[512,1536]{1,0:T(8,128)(2,1)} async-done(((bf16[512,1536]{1,0:T(8,128)(2,1)}), bf16[512,1536]{1,0:T(8,128)(2,1)}) %all-reduce.8.cloned.1.call-update) | async-done | bytes 1572880 | tf_op jit(solution)/shard_map/psum | solution.py:132
  156.3 6.5 fusion.77
  162.9 4.9 fusion.76
  167.8 10.1 multiply_convert_fusion
  177.9 5.2 fusion.78
  183.2 7.6 fusion.34
  191.0 21.5 %all-reduce.10.cloned.1.call-done = bf16[512,1536]{1,0:T(8,128)(2,1)} async-done(((bf16[512,1536]{1,0:T(8,128)(2,1)}), bf16[512,1536]{1,0:T(8,128)(2,1)}) %all-reduce.10.cloned.1.call-update) | async-done | bytes 1572880 | tf_op jit(solution)/shard_map/psum | solution.py:158
  212.5 3.7 fusion.22
  225.7 15.2 %bitcast_convert_fusion = bf16[4,96,2048]{2,1,0:T(8,128)(2,1)} fusion(bf16[512,4,2,96]{0,3,2,1:T(8,128)(2,1)S(1)} %bitcast.212, f32[4,2048,512,2]{2,1,3,0:T(8,128)} %get-tuple-element.139, f32[4,2,512]{2,1,0:T(2,128)S(1)} %bitcast.233, pred[512,2048]{0,1:T(8,128)(4,1)S(1)} %fusion.5), kind=kOutput, calls=%fused_computation.55 | convolution fusion | flops 1644953600 | bytes 36978688 | tf_op jit(solution)/shard_map/while/body/eval_jaxpr/while/body/eval_jaxpr/kgqs,qkgd->skd/dot_general | solution.py:216
  240.9 20.1 %fusion.1 = bf16[4,2,512,2048]{2,3,1,0:T(8,128)(2,1)} fusion(f32[4,2048,512,2]{2,1,3,0:T(8,128)} %get-tuple-element.139, bf16[2048,4,96,1]{0,2,3,1:T(8,128)(2,1)S(1)} %bitcast.218, bf16[512,4,2,96]{0,3,2,1:T(8,128)(2,1)S(1)} %bitcast.213, f32[4,2,512]{2,1,0:T(2,128)S(1)} %bitcast.231, f32[4,2,512]{2,1,0:T(2,128)S(1)} %bitcast.234, ...), kind=kOutput, calls=%fused_computation.2 | convolution fusion | flops 1660944384 | bytes 53772288 | tf_op jit(solution)/shard_map/while/body/eval_jaxpr/while/body/eval_jaxpr/qkgd,skd->kgqs/dot_general | solution.py:200
  261.0 11.2 fusion.32
  276.0 8.1 convolution_convert_fusion.5
  284.1 8.5 convolution_multiply_fusion
  297.7 39.8 %reduce-scatter.2.cloned.1.call-done = bf16[1,512,768]{1,2,0:T(8,128)(2,1)} async-done(((bf16[1,2048,768]{1,2,0:T(8,128)(2,1)}), bf16[1,512,768]{1,2,0:T(8,128)(2,1)}) %reduce-scatter.2.cloned.1.call-update) | async-done | bytes 786448 | tf_op jit(solution)/shard_map/reduce_scatter | solution.py:232
  345.5 7.1 convolution_convert_fusion.1
  352.6 5.3 convolution_convert_fusion.2
  358.0 5.4 convolution_convert_fusion
  377.3 45.3 %all-reduce = (bf16[1536]{0:T(1024)(128)(2,1)S(1)}, bf16[1536]{0:T(1024)(128)(2,1)S(1)}) all-reduce(bf16[1536]{0:T(1024)(128)(2,1)S(1)} %get-tuple-element.94, bf16[1536]{0:T(1024)(128)(2,1)S(1)} %get-tuple-element.92), channel_id=1, replica_groups=mesh['dp'=4,'ctx'=4,'tensor'=2] {'dp','ctx'}, use_global_device_ids=true, to_apply=%region_13.14 | all-reduce | flops 3072 | bytes 12288 | tf_op jit(solution)/shard_map/psum | solution.py:280
  423.8 5.2 fusion.38
  429.1 567.7 %all-reduce.12.cloned.1.call-done = (bf16[1536,384]{1,0:T(8,128)(2,1)}, bf16[1536,384]{1,0:T(8,128)(2,1)}, bf16[768,1536]{1,0:T(8,128)(2,1)}, bf16[1536,2048]{1,...) async-done(((bf16[1536,384]{1,0:T(8,128)(2,1)}, bf16[1536,384]{1,0:T(8,128)(2,1)}, bf16[768,1536]{1,0:T(8,128)(2,1)}, bf16[1536,2048]{1,0:T(8,128)(2,1)}, ...) | async-done | bytes 23592976 | tf_op jit(solution)/shard_map/psum | solution.py:282
  1004.2 10.0 convert_element_type.296
  1014.2 6.3 convert_element_type.298
  1020.5 6.6 convert_element_type.300
  1027.1 362.2 %all-gather.6.cloned.1.call-done = bf16[24576,768]{1,0:T(8,128)(2,1)} async-done(((bf16[1536,768]{1,0:T(8,128)(2,1)}), bf16[24576,768]{1,0:T(8,128)(2,1)}) %all-gather.6.cloned.1.call-update) | async-done | bytes 37748752 | tf_op jit(solution)/shard_map/all_gather | solution.py:281
  1389.3 14.8 %reduce_sum.94 = bf16[1536,768]{1,0:T(8,128)(2,1)} reduce(bf16[16,1536,768]{2,1,0:T(8,128)(2,1)} %bitcast.199, bf16[]{:T(256)} %constant.163.clone.1), dimensions={0}, to_apply=%region_14.15 | reduce | flops 17694720 | bytes 40108032 | tf_op jit(solution)/shard_map/reduce_sum | solution.py:281
  1404.1 4.2 convert_element_type.286
  (167 shorter events, 72.3 us)
Async XLA Ops:
  7.2 124.0 %copy-start = (bf16[768,1536]{1,0:T(8,128)(2,1)S(1)}, bf16[768,1536]{1,0:T(8,128)(2,1)}, u32[]{:S(2)}) copy-start(bf16[768,1536]{1,0:T(8,128)(2,1)} %param.21) | copy-start | bytes 7077892
  7.2 77.6 %all-gather.4.cloned.1.call-start = ((), (), s32[]{:S(2)}) async-start(), calls=%async_computation.1 | async-start | bytes 3932160 | tf_op jit(solution)/shard_map/all_gather | solution.py:104
  10.9 12.2 copy-start.37
  17.3 9.4 copy-start.16
  18.4 134.4 %all-reduce.8.cloned.1.call-start = ((), (), s32[]{:S(2)}) async-start(), calls=%async_computation.2 | async-start | bytes 3145728 | tf_op jit(solution)/shard_map/psum | solution.py:132
  87.0 13.8 copy-start.10
  87.0 28.2 %copy-start.22 = (bf16[2048,384]{0,1:T(8,128)(2,1)}, bf16[2048,384]{0,1:T(8,128)(2,1)S(1)}, u32[]{:S(2)}) copy-start(bf16[2048,384]{0,1:T(8,128)(2,1)S(1)} %get-tuple-element.120) | copy-start | bytes 4718596
  133.7 21.8 %copy-start.34 = (f32[1536]{0:T(1024)S(1)}, f32[1536]{0:T(1024)}, u32[]{:S(2)}) copy-start(f32[1536]{0:T(1024)} %param.22) | copy-start | bytes 18436
  133.7 78.8 %all-reduce.10.cloned.1.call-start = ((), (), s32[]{:S(2)}) async-start(), calls=%async_computation.3 | async-start | bytes 3145728 | tf_op jit(solution)/shard_map/psum | solution.py:158
  155.7 7.1 slice-start.4
  156.3 6.5 copy-start.20
  156.3 6.5 slice-start.5
  190.8 146.7 %reduce-scatter.2.cloned.1.call-start = ((), (), s32[]{:S(2)}) async-start(), calls=%async_computation.4 | async-start | bytes 3932160 | tf_op jit(solution)/shard_map/reduce_scatter | solution.py:232
  225.7 15.3 %copy-start.23 = (bf16[2048,384]{0,1:T(8,128)(2,1)S(1)}, bf16[2048,384]{0,1:T(8,128)(2,1)}, u32[]{:S(2)}) copy-start(bf16[2048,384]{0,1:T(8,128)(2,1)} %copy-done.22) | copy-start | bytes 4718596
  275.7 99.0 %all-reduce.14.cloned.1.call-start = ((), (), s32[]{:S(2)}) async-start(), calls=%async_computation.7 | async-start | bytes 6291456 | tf_op jit(solution)/shard_map/psum | solution.py:143
  276.0 8.1 copy-start.11
  284.1 8.5 copy-start.17
  284.1 8.5 copy-start.30
  297.7 41.1 %copy-start.13 = (bf16[1536,384]{1,0:T(8,128)(2,1)S(1)}, bf16[1536,384]{1,0:T(8,128)(2,1)}, u32[]{:S(2)}) copy-start(bf16[1536,384]{1,0:T(8,128)(2,1)} %param.19) | copy-start | bytes 3538948
  344.1 652.6 %all-reduce.12.cloned.1.call-start = ((), (), s32[]{:S(2)}) async-start(), calls=%async_computation.6 | async-start | bytes 47185920 | tf_op jit(solution)/shard_map/psum | solution.py:282
  345.5 7.1 copy-start.42
  352.6 5.4 copy-start.25
  352.6 5.4 copy-start.44
  358.0 5.4 copy-start.9
  358.0 5.4 copy-start.15
  370.6 1018.7 %all-gather.6.cloned.1.call-start = ((), (), s32[]{:S(2)}) async-start(), calls=%async_computation.5 | async-start | bytes 40108032 | tf_op jit(solution)/shard_map/all_gather | solution.py:281
  374.7 49.2 %copy-start.40 = (f32[512]{0:T(512)S(1)}, f32[512]{0:T(512)}, u32[]{:S(2)}) copy-start(f32[512]{0:T(512)} %get-tuple-element.134) | copy-start | bytes 6148
  1001.3 12.9 slice-start.2
  1004.2 10.0 slice-start.3
  1004.2 16.3 %slice-start = ((s8[6291456]{0:T(1024)(128)(4,1)}), s8[4194304]{0:T(1024)(128)(4,1)S(1)}, s32[]{:S(2)}) async-start(s8[6291456]{0:T(1024)(128)(4,1)} %bitcast.204), calls=%async_computation.8 | async-start | bytes 8388608
  1014.2 6.3 slice-start.1
  1389.3 19.0 %copy-start.1 = (bf16[768,1536]{1,0:T(8,128)(2,1)S(1)}, bf16[768,1536]{1,0:T(8,128)(2,1)}, u32[]{:S(2)}) copy-start(bf16[768,1536]{1,0:T(8,128)(2,1)} %param.21) | copy-start | bytes 7077892
  (26 other events, 75.1 us)
Sparse Core Ops, SparseCore 0:
  18.6 66.1 all-gather.3
  133.8 19.0 all-reduce.7
  190.9 21.5 all-reduce.9
  275.8 61.5 reduce-scatter.1
  344.2 23.2 all-reduce.13
  374.9 621.7 all-reduce.11
  1000.1 389.1 all-gather.5
